TPU v7x, 128 devices: a whole 4x4x4 slice. The times are simulated.
128 devices in a mesh: grp: 64 (over x, z, y), rep: 2 (over core).
Axes of the slice: x: 4, y: 4, z: 4, core: 2. Of those that a mesh axis runs over, the one named last changes fastest.
Arguments:
- states: float32 [16384, 1024], P(('grp', 'rep')), may hold values from 0 to 1
- coupling: bfloat16 [1024, 2048], replicated, may hold values from -0.1875 to 0.1875
- vis_bias: float32 [1024], replicated, may hold values from -6 to 6
- hid_bias: float32 [2048], replicated, may hold values from -6 to 6
- noise: bfloat16 [4, 16384, 2048], P(None, ('grp', 'rep')), may hold values from -6 to 6
- tickets: int32 [16384], P(('grp', 'rep')), may hold values from 1 to 4
- offset: int32 [1], replicated, may hold values from 0 to 16383
Outputs:
- visible: float32 [16384, 1024], P(('grp', 'rep'))
- weights: float32 [16384], P(('grp', 'rep'))
- log_ratio: float32 [], replicated
All inputs are finite; a program needn't handle non-finite values.
Results may differ from a plain program's by a relative error of at most 0.0047.
Values may be sent and summed in bfloat16 or wider, within the bound.
A program may use at most 64 MiB of HBM per device.

v0:
```python
import jax
import jax.numpy as jnp
from jax import lax
from jax.sharding import Mesh
from jax.sharding import PartitionSpec as P

SWEEPS = 4
GRP_REP = ("grp_0", "grp_1", "grp_2", "rep")


def copy_for_each(array, axis):
    length = lax.axis_size(axis)
    return lax.all_to_all(
        jnp.broadcast_to(array[None], (length, *array.shape)), axis, 0, 0, tiled=True
    )


def laid_out(parts, dim):
    parts = jnp.moveaxis(parts, 0, dim)
    dims = parts.shape
    return parts.reshape(*dims[:dim], dims[dim] * dims[dim + 1], *dims[dim + 2 :])


def gather_axes(array, axes, dim):
    far, near = axes
    initial = copy_for_each(array, far)
    parts = jnp.swapaxes(copy_for_each(initial, near), 0, 1)
    return laid_out(parts.reshape(-1, *array.shape), dim)


def side_by_side(arrays, axis, split_dim, concat_dim, along):
    columns = [a.reshape(*a.shape[:along], -1) for a in arrays]
    both = jnp.concatenate(columns, axis=along)
    filled, at, finished = (
        lax.all_to_all(both, axis, split_axis=split_dim, concat_axis=concat_dim, tiled=True),
        0,
        [],
    )
    for a, column in zip(arrays, columns):
        section = filled[..., at : at + column.shape[along]]
        finished.append(section.reshape(*section.shape[:along], *a.shape[along:]))
        at += column.shape[along]
    return tuple(finished)


def over_copies(array, axis):
    return copy_for_each(array, axis).max(axis=0)


def one_axis_at_a_time(array, axes):
    far, near = axes
    return over_copies(over_copies(array, near), far)


def of_everyone(array, axis):
    everything = copy_for_each(array, axis)
    return jnp.sum(everything, axis=0)


def one_axis_at_a_time_2(array, axes):
    far, near = axes
    nearer = of_everyone(array, near)
    return of_everyone(nearer, far)


def per_device(states, coupling, vis_bias, hid_bias, noise, tickets, offset):
    devices = lax.axis_size(GRP_REP)
    myself = lax.axis_index(GRP_REP)
    local_rows = states.shape[0]
    width = states.shape[1]
    chains = local_rows * devices
    beta_step = 204.8 / coupling.shape[1]
    own_total = jnp.sum(tickets)
    every = gather_axes(own_total[None], (("grp_0", "grp_1", "grp_2"), "rep"), 0)
    grand_total = jnp.sum(every)
    before = jnp.sum(jnp.where(jnp.arange(devices, dtype=jnp.int32) < myself, every, 0))
    jitter = offset[0]

    def first_slot(levels):
        return jnp.clip(-((jitter - levels * chains) // grand_total), 0, chains)

    ends = first_slot(before + jnp.cumsum(tickets))
    opening = first_slot(before)
    closing = ends[-1]
    capacity = -(-4 * local_rows // devices)
    target = jnp.arange(devices, dtype=jnp.int32)[:, None]
    lanes = jnp.arange(capacity, dtype=jnp.int32)[None, :]
    slot_ids = opening + (target - opening) % devices + lanes * devices
    filled = slot_ids < closing
    chosen = jnp.sum((ends[None, None, :] <= slot_ids[:, :, None]).astype(jnp.int32), axis=-1)
    chosen = jnp.minimum(chosen, local_rows - 1)
    outgoing = jnp.where(filled[:, :, None], jnp.take(states, chosen, axis=0), 0.0).astype(
        jnp.bfloat16
    )
    labels = jnp.where(filled, slot_ids // devices + 1, 0).astype(jnp.bfloat16)
    arrived, arrived_labels = side_by_side((outgoing, labels), GRP_REP, 0, 0, 2)
    arrived = arrived.reshape(devices * capacity, width)
    arrived_labels = arrived_labels.reshape(devices * capacity).astype(jnp.float32)
    selector = (
        arrived_labels[None, :] == (jnp.arange(local_rows, dtype=jnp.float32) + 1.0)[:, None]
    ).astype(jnp.bfloat16)
    visible_b = jnp.dot(selector, arrived, preferred_element_type=jnp.float32).astype(jnp.bfloat16)
    visible = visible_b.astype(jnp.float32)
    for sweep_idx in range(SWEEPS):
        pre_hidden = jnp.dot(visible_b, coupling, preferred_element_type=jnp.float32)
        hidden = jax.nn.sigmoid(
            pre_hidden + hid_bias + noise[sweep_idx].astype(jnp.float32)
        ).astype(jnp.bfloat16)
        pre_visible = lax.dot_general(
            hidden, coupling, (((1,), (1,)), ((), ())), preferred_element_type=jnp.float32
        )
        visible = 0.5 * visible + 0.5 * jax.nn.sigmoid(pre_visible + vis_bias)
        visible_b = visible.astype(jnp.bfloat16)
    activity = jnp.dot(visible_b, coupling, preferred_element_type=jnp.float32) + hid_bias
    log_weight = beta_step * (
        jnp.sum(visible * vis_bias, axis=-1) + jnp.sum(jax.nn.softplus(activity), axis=-1)
    )
    highest = one_axis_at_a_time(jnp.max(log_weight), (("grp_0", "grp_1", "grp_2"), "rep"))
    mass_sum = one_axis_at_a_time_2(
        jnp.sum(jnp.exp(log_weight - highest)), (("grp_0", "grp_1", "grp_2"), "rep")
    )
    weights = jnp.exp(log_weight - highest) * (chains / mass_sum)
    log_ratio = highest + jnp.log(mass_sum) - jnp.log(jnp.float32(chains))
    return (visible, weights, log_ratio)


def solution(mesh):
    finer = Mesh(
        mesh.devices.reshape(4, 4, 4, mesh.shape["rep"]), ("grp_0", "grp_1", "grp_2", "rep")
    )
    return jax.shard_map(
        per_device,
        mesh=finer,
        in_specs=(P(GRP_REP, None), P(), P(), P(), P(None, GRP_REP, None), P(GRP_REP), P()),
        out_specs=(P(GRP_REP, None), P(GRP_REP), P()),
        check_vma=False,
    )
```

profile of v0, /device:TPU:0, one launch (start us, length us, event | category | flops | bytes accessed | tf_op | source)
XLA Modules:
  0.0 147.7 jit_solution(16745365141974890135)
XLA Ops:
  0.6 1.4 reduce_sum.81
  2.0 1.3 broadcast_in_dim.42
  3.3 11.5 %all-to-all-start = ((s32[64,1,1]{2,1,0:T(1,128)}), s32[64,1,1]{2,1,0:T(1,128)S(1)}, u32[]{:S(2)}, u32[]{:S(2)}) async-start(s32[64,1,1]{2,1,0:T(1,128)} %broadcast_in_dim.42), calls=%async_computation | async-start | bytes 65536 | tf_op jit(solution)/shard_map/all_to_all | solution.py:13
  15.5 0.8 copy.42
  16.4 7.9 %all-to-all-done = s32[64,1,1]{2,1,0:T(1,128)S(1)} async-done(((s32[64,1,1]{2,1,0:T(1,128)}), s32[64,1,1]{2,1,0:T(1,128)S(1)}, u32[]{:S(2)}, u32[]{:S(2)}) %all-to-all-start) | async-done | bytes 288 | tf_op jit(solution)/shard_map/all_to_all | solution.py:13
  24.3 1.2 reduce.7
  25.5 3.7 %all_to_all.40 = s32[2,64,1]{1,2,0:T(1,128)S(1)} all-to-all(s32[2,64,1]{1,2,0:T(1,128)S(1)} %broadcast_in_dim.44), channel_id=1, replica_groups=mesh['grp_0'=4,'grp_1'=4,'grp_2'=4,'rep'=2] {'rep'}, dimensions={0} | all-to-all | bytes 1024 | tf_op jit(solution)/shard_map/all_to_all | solution.py:13
  33.2 2.1 %fusion.74 = pred[128]{0:T(512)(128)(4,1)S(1)} fusion(s32[128,1]{1,0:T(8,128)S(1)} %reduce-window.7, s32[]{:T(128)S(6)} %sign.35, s32[]{:T(128)} %reduce_sum.83, s32[]{:T(128)} %fusion.81, s32[]{:T(128)} %bitcast.49), kind=kLoop, calls=%fused_computation.94 | loop fusion | flops 1024 | bytes 656 | tf_op jit(solution)/shard_map/jit(floor_divide)/and | solution.py:80
  35.2 2.0 %divide_reduce_fusion = s32[128]{0:T(128)S(1)} fusion(s32[128,1]{1,0:T(8,128)S(1)} %reduce-window.7, s32[]{:T(128)} %reduce_sum.83, s32[]{:T(128)} %fusion.81, s32[]{:T(128)} %bitcast.50), kind=kLoop, calls=%fused_computation.92 | loop fusion | flops 512 | bytes 1036 | tf_op jit(solution)/shard_map/jit(floor_divide)/div | solution.py:80
  38.2 0.7 broadcast_compare_fusion
  38.9 0.7 fusion.78
  40.4 1.8 %gather_fusion = bf16[512,1024]{1,0:T(8,128)(2,1)S(1)} fusion(f32[128,1024]{1,0:T(8,128)S(1)} %copy-done, s32[1024]{0:T(1024)S(1)} %pad_clamp_fusion), kind=kCustom, calls=%fused_computation | custom fusion | bytes 2099200 | tf_op jit(solution)/shard_map/jit(_take)/gather | solution.py:92
  42.6 1.0 select_convert_fusion
  43.6 1.6 %pad_maximum_fusion = bf16[128,4,1025]{2,1,0:T(4,128)(2,1)} fusion(bf16[128,4,1]{2,1,0:T(4,128)(2,1)S(1)} %copy.46, bf16[128,4,1024]{2,1,0:T(4,128)(2,1)S(1)} %select_convert_fusion), kind=kLoop, calls=%fused_computation.59 | loop fusion | flops 2099200 | bytes 2099200 | tf_op jit(solution)/shard_map/concatenate | solution.py:33
  45.2 4.9 %all-to-all-start.2 = ((bf16[128,4,1025]{2,1,0:T(4,128)(2,1)}), bf16[128,4,1025]{2,1,0:T(4,128)(2,1)S(1)}, u32[]{:S(2)}, u32[]{:S(2)}) async-start(bf16[128,4,1025]{2,1,0:T(4,128)(2,1)} %pad_maximum_fusion), calls=%async_computation.2 | async-start | bytes 2359296 | tf_op jit(solution)/shard_map/all_to_all | solution.py:35
  50.1 20.4 %all-to-all-done.2 = bf16[128,4,1025]{2,1,0:T(4,128)(2,1)S(1)} async-done(((bf16[128,4,1025]{2,1,0:T(4,128)(2,1)}), bf16[128,4,1025]{2,1,0:T(4,128)(2,1)S(1)}, u32[]{:S(2)}, u32[]{:S(2)}) %all-to-all-start.2) | async-done | bytes 1049632 | tf_op jit(solution)/shard_map/all_to_all | solution.py:35
  71.9 6.7 %fusion.43 = f32[128,1024]{1,0:T(8,128)} fusion(bf16[1024,2048]{1,0:T(8,128)(2,1)} %param.8, bf16[128,1024]{1,0:T(8,128)(2,1)S(1)} %convolution_convert_fusion, bf16[4,128,2048]{2,1,0:T(8,128)(2,1)} %param.11, f32[2048]{0:T(1024)S(1)} %copy-done.2, f32[1024]{0:T(1024)S(1)} %copy-done.3), kind=kOutput, calls=%fused_computation.55 | convolution fusion | flops 1076363264 | bytes 9973760 | tf_op jit(solution)/shard_map/dot_general | solution.py:109
  78.5 6.2 %fusion.45 = f32[128,1024]{1,0:T(8,128)S(1)} fusion(bf16[1024,2048]{1,0:T(8,128)(2,1)} %param.8, bf16[4,128,2048]{2,1,0:T(8,128)(2,1)} %param.11, f32[128,1024]{1,0:T(8,128)} %fusion.43, f32[2048]{0:T(1024)S(1)} %copy-done.2, f32[1024]{0:T(1024)S(1)} %copy-done.3), kind=kOutput, calls=%fused_computation.57 | convolution fusion | flops 1076756480 | bytes 10498048 | tf_op jit(solution)/shard_map/dot_general | solution.py:109
  84.7 6.5 %fusion.42 = f32[128,1024]{1,0:T(8,128)} fusion(f32[128,1024]{1,0:T(8,128)S(1)} %fusion.45, bf16[1024,2048]{1,0:T(8,128)(2,1)} %param.8, bf16[4,128,2048]{2,1,0:T(8,128)(2,1)S(1)} %copy-done.1, f32[2048]{0:T(1024)S(1)} %copy-done.2, f32[1024]{0:T(1024)S(1)} %copy-done.3), kind=kOutput, calls=%fused_computation.54 | convolution fusion | flops 1076363264 | bytes 10498048 | tf_op jit(solution)/shard_map/dot_general | solution.py:109
  91.2 6.0 %multiply_reduce_fusion = (f32[128]{0:T(128)S(1)}, f32[128,1024]{1,0:T(8,128)S(1)}) fusion(f32[1024]{0:T(1024)S(1)} %copy-done.3, bf16[1024,2048]{1,0:T(8,128)(2,1)} %param.8, bf16[4,128,2048]{2,1,0:T(8,128)(2,1)S(1)} %copy-done.1, f32[2048]{0:T(1024)S(1)} %copy-done.2, f32[128,1024]{1,0:T(8,128)} %fusion.42), kind=kOutput, calls=%fused_computation.65 | convolution fusion | flops 1077018496 | bytes 10498560 | tf_op jit(solution)/shard_map/dot_general | solution.py:109
  97.2 3.7 %fusion.46 = f32[128]{0:T(128)S(1)} fusion(bf16[1024,2048]{1,0:T(8,128)(2,1)} %param.8, f32[2048]{0:T(1024)S(1)} %copy-done.2, f32[128,1024]{1,0:T(8,128)S(1)} %get-tuple-element.6), kind=kOutput, calls=%fused_computation.60 | convolution fusion | flops 539099008 | bytes 4727296 | tf_op jit(solution)/shard_map/dot_general | solution.py:114
  101.5 0.6 broadcast_in_dim.50
  102.2 3.7 %all_to_all.41 = f32[2,1,1]{2,1,0:T(1,128)S(1)} all-to-all(f32[2,1,1]{2,1,0:T(1,128)S(1)} %broadcast_in_dim.50), channel_id=1, replica_groups=mesh['grp_0'=4,'grp_1'=4,'grp_2'=4,'rep'=2] {'rep'}, dimensions={0} | all-to-all | bytes 16 | tf_op jit(solution)/shard_map/all_to_all | solution.py:13
  106.5 0.7 broadcast_in_dim.51
  107.2 14.3 %all_to_all.42 = f32[64,1,1]{2,1,0:T(1,128)S(1)} all-to-all(f32[64,1,1]{2,1,0:T(1,128)S(1)} %broadcast_in_dim.51), channel_id=1, replica_groups=mesh['grp_0'=4,'grp_1'=4,'grp_2'=4,'rep'=2] {'grp_0','grp_1','grp_2'}, dimensions={0} | all-to-all | bytes 512 | tf_op jit(solution)/shard_map/all_to_all | solution.py:13
  121.4 0.7 reduce_max.29
  122.1 1.3 fusion.95
  123.4 0.6 broadcast_in_dim.52
  124.0 3.7 %all_to_all.43 = f32[2,1,1]{2,1,0:T(1,128)S(1)} all-to-all(f32[2,1,1]{2,1,0:T(1,128)S(1)} %broadcast_in_dim.52), channel_id=1, replica_groups=mesh['grp_0'=4,'grp_1'=4,'grp_2'=4,'rep'=2] {'rep'}, dimensions={0} | all-to-all | bytes 16 | tf_op jit(solution)/shard_map/all_to_all | solution.py:13
  128.3 0.7 broadcast_in_dim.53
  129.0 14.3 %all_to_all.44 = f32[64,1,1]{2,1,0:T(1,128)S(1)} all-to-all(f32[64,1,1]{2,1,0:T(1,128)S(1)} %broadcast_in_dim.53), channel_id=1, replica_groups=mesh['grp_0'=4,'grp_1'=4,'grp_2'=4,'rep'=2] {'grp_0','grp_1','grp_2'}, dimensions={0} | all-to-all | bytes 512 | tf_op jit(solution)/shard_map/all_to_all | solution.py:13
  143.3 0.7 reduce_sum.89
  (39 shorter events, 7.2 us)
Async XLA Ops:
  0.6 39.7 %copy-start = (f32[128,1024]{1,0:T(8,128)S(1)}, f32[128,1024]{1,0:T(8,128)}, u32[]{:S(2)}) copy-start(f32[128,1024]{1,0:T(8,128)} %param.7) | copy-start | bytes 1572868
  3.3 21.0 %all-to-all-start = ((s32[64,1,1]{2,1,0:T(1,128)}), s32[64,1,1]{2,1,0:T(1,128)S(1)}, u32[]{:S(2)}, u32[]{:S(2)}) async-start(s32[64,1,1]{2,1,0:T(1,128)} %broadcast_in_dim.42), calls=%async_computation | async-start | bytes 65536 | tf_op jit(solution)/shard_map/all_to_all | solution.py:13
  45.2 26.7 %copy-start.2 = (f32[2048]{0:T(1024)S(1)}, f32[2048]{0:T(1024)}, u32[]{:S(2)}) copy-start(f32[2048]{0:T(1024)} %param.10) | copy-start | bytes 24580
  45.2 26.7 %copy-start.3 = (f32[1024]{0:T(1024)S(1)}, f32[1024]{0:T(1024)}, u32[]{:S(2)}) copy-start(f32[1024]{0:T(1024)} %param.9) | copy-start | bytes 12292
  45.2 25.3 %all-to-all-start.2 = ((bf16[128,4,1025]{2,1,0:T(4,128)(2,1)}), bf16[128,4,1025]{2,1,0:T(4,128)(2,1)S(1)}, u32[]{:S(2)}, u32[]{:S(2)}) async-start(bf16[128,4,1025]{2,1,0:T(4,128)(2,1)} %pad_maximum_fusion), calls=%async_computation.2 | async-start | bytes 2359296 | tf_op jit(solution)/shard_map/all_to_all | solution.py:35
  78.5 6.2 %copy-start.1 = (bf16[4,128,2048]{2,1,0:T(8,128)(2,1)S(1)}, bf16[4,128,2048]{2,1,0:T(8,128)(2,1)}, u32[]{:S(2)}) copy-start(bf16[4,128,2048]{2,1,0:T(8,128)(2,1)} %param.11) | copy-start | bytes 6291460
  97.2 49.3 %copy-start.4 = (f32[128,1024]{1,0:T(8,128)}, f32[128,1024]{1,0:T(8,128)S(1)}, u32[]{:S(2)}) copy-start(f32[128,1024]{1,0:T(8,128)S(1)} %get-tuple-element.6) | copy-start | bytes 1572868
where the time goes:
time: 148 us
  blocking collectives  39.7 us (27%)
  matrix products  29.4 us (20%)
  waiting for transfers between devices  28.3 us (19%)
  other arithmetic  17.6 us (12%)
  starting transfers between devices  16.5 us (11%)
  local copies, waits for them, and re-layouts  8.93 us (6%)
  between operations  7.31 us (5%)
    all_to_all x5, blocking collectives, copy_for_each(): lax.all_to_all(jnp.broadcast_to(array[None], (length, *array.shape)), axi...  39.7 us
    dot_general x4, matrix products, per_device(): lax.dot_general(hidden, coupling, (((1,), (1,)), ((), ())), preferred_ele...  25.3 us
    all_to_all x1, waiting for transfers between devices, side_by_side(): lax.all_to_all(both, axis, split_axis=split_dim, concat_axis=concat_dim,...  20.4 us
    all_to_all x1, starting transfers between devices, copy_for_each(): lax.all_to_all(jnp.broadcast_to(array[None], (length, *array.shape)), axi...  11.5 us
    all_to_all x1, waiting for transfers between devices, copy_for_each(): lax.all_to_all(jnp.broadcast_to(array[None], (length, *array.shape)), axi...  7.89 us
    all_to_all x1, starting transfers between devices, side_by_side(): lax.all_to_all(both, axis, split_axis=split_dim, concat_axis=concat_dim,...  4.94 us
    broadcast_in_dim x6, local copies, waits for them, and re-layouts, copy_for_each(): jnp.broadcast_to(array[None], (length, *array.shape))  3.9 us
    dot_general x1, matrix products, per_device(): jnp.dot(visible_b, coupling, preferred_element_type=jnp.float32) + hid_bias  3.7 us
  transfers between devices with their start and end apart: 2, of which 2 were waited for; matrix products, arithmetic and copies ran while one was open for 1% of the time, Pallas kernels for 0%

commit v1 on v0

v1 whole, which is shorter than its diff:
```python
import jax
import jax.numpy as jnp
from jax import lax
from jax.experimental import pallas as pl
from jax.experimental.pallas import tpu as pltpu
from jax.sharding import PartitionSpec as P

MESH = pl.DeviceIdType.MESH
SWEEPS = 4
ROWS = 128
GROUP = 8
GROUPS = 16
CAP = 32
SHIFT = 14
CHAINS = 1 << SHIFT


def where_is(t):
    return (t // 2, lax.rem(t, 2))


def remote(src, dst, send, recv, t):
    return pltpu.make_async_remote_copy(
        src_ref=src,
        dst_ref=dst,
        send_sem=send,
        recv_sem=recv,
        device_id=where_is(t),
        device_id_type=MESH,
    )


def wait_bytes(ref, sem):
    pltpu.make_async_copy(ref, ref, sem).wait()


def logistic(x):
    return 0.5 * jnp.tanh(0.5 * x) + 0.5


def step_kernel(
    states_ref,
    coupling_ref,
    vis_bias_ref,
    hid_bias_ref,
    noise_ref,
    tickets_ref,
    offset_ref,
    visible_ref,
    weights_ref,
    ratio_ref,
    own_tickets,
    group_tickets,
    all_tickets,
    vis,
    pool,
    onehot,
    outbox,
    inbox,
    cpl,
    cpl_t,
    nz,
    hb,
    vb,
    hid,
    visb,
    own_stat,
    group_stats,
    all_stats,
    load_sems,
    tick_sems,
    ring_send,
    ring_recv,
    pair_send,
    pair_recv,
    rows_send,
    rows_recv,
    stat_sems,
    out_sem,
):
    me = lax.axis_index("grp") * 2 + lax.axis_index("rep")
    core = lax.rem(me, 2)
    seat = lax.rem(me, GROUP)
    line = lax.rem(me // 2, 4)
    group = me // GROUP
    gx, gz = group // 4, lax.rem(group, 4)
    base = me - seat
    sibling = me + 1 - 2 * core
    up = base + 2 * lax.rem(line + 1, 4) + core
    down = base + 2 * lax.rem(line + 3, 4) + core
    mates = [base + lax.rem(seat + i, GROUP) for i in range(1, GROUP)]

    def plane(i):
        return 4 * lax.rem(gx + i // 4, 4) + lax.rem(gz + i % 4, 4)

    rows = [GROUP * plane(i) + seat for i in range(1, GROUPS)]

    barrier = pltpu.get_barrier_semaphore()
    for t in mates + rows:
        pl.semaphore_signal(barrier, inc=1, device_id=where_is(t), device_id_type=MESH)

    loads = [
        pltpu.make_async_copy(src, dst, load_sems.at[i])
        for i, (src, dst) in enumerate(
            (
                (tickets_ref, own_tickets),
                (states_ref, vis),
                (coupling_ref, cpl),
                (noise_ref, nz),
                (hid_bias_ref, hb),
                (vis_bias_ref, vb),
            )
        )
    ]
    for copy in loads:
        copy.start()
    loads[0].wait()
    group_tickets[pl.ds(seat, 1), :] = own_tickets[...]
    loads[1].wait()

    def block(owner, half=None):
        if half is None:
            return pool.at[pl.ds(pl.multiple_of(owner * ROWS, ROWS), ROWS)]
        start = pl.multiple_of(owner * ROWS + half * (ROWS // 2), ROWS // 2)
        return pool.at[pl.ds(start, ROWS // 2)]

    pool[pl.ds(pl.multiple_of(seat * ROWS, ROWS), ROWS), :] = vis[...].astype(jnp.bfloat16)
    pl.semaphore_wait(barrier, GROUP - 1 + GROUPS - 1)

    for t in mates:
        remote(
            own_tickets, group_tickets.at[pl.ds(seat, 1)], tick_sems.at[0], tick_sems.at[1], t
        ).start()
    sends = []

    def ring(owner, half, to_up, slot):
        copy = remote(
            block(owner, half),
            block(owner, half),
            ring_send.at[slot],
            ring_recv.at[slot],
            up if to_up else down,
        )
        copy.start()
        sends.append(copy)

    def hand(owner, half, slot):
        copy = remote(
            block(owner, half), block(owner, half), pair_send.at[slot], pair_recv, sibling
        )
        copy.start()
        sends.append(copy)

    prev = lax.rem(seat + 6, GROUP)
    after = lax.rem(seat + 2, GROUP)
    across = lax.rem(seat + 4, GROUP)
    ring(seat, 0, True, 0)
    ring(seat, 1, False, 1)
    ring(seat, 1, True, 2)
    ring(seat, 0, False, 3)
    hand(seat, None, 0)

    wait_bytes(group_tickets.at[pl.ds(0, GROUP - 1)], tick_sems.at[1])
    my_rows = pl.ds(pl.multiple_of(base, GROUP), GROUP)
    all_tickets[my_rows, :] = group_tickets[...]
    for t in rows:
        remote(
            group_tickets, all_tickets.at[my_rows], tick_sems.at[2], tick_sems.at[3], t
        ).start()

    wait_bytes(block(prev, 0), ring_recv.at[0])
    ring(prev, 0, True, 4)
    hand(prev, 0, 1)
    wait_bytes(block(after, 1), ring_recv.at[1])
    ring(after, 1, False, 5)
    hand(after, 1, 2)

    wait_bytes(all_tickets.at[pl.ds(0, (GROUPS - 1) * GROUP)], tick_sems.at[3])
    everything = all_tickets[...].astype(jnp.float32)
    totals = jnp.sum(everything, axis=1, keepdims=True)
    grand = jnp.sum(totals, axis=0, keepdims=True).astype(jnp.int32)
    z_high, z_low = grand >> SHIFT, grand & (CHAINS - 1)
    jitter = offset_ref[0]

    def point(k):
        return k * z_high + ((k * z_low + jitter) >> SHIFT)

    def count(mask, axis):
        return jnp.sum(jnp.where(mask, 1.0, 0.0), axis=axis, keepdims=True).astype(jnp.int32)

    device = lax.broadcasted_iota(jnp.int32, (ROWS, 1), 0)
    before = jnp.sum(jnp.where(device < base, totals, 0.0), axis=0, keepdims=True)
    group_first = before.astype(jnp.int32)

    slot_row = lax.broadcasted_iota(jnp.int32, (GROUPS * CAP, 1), 0)
    turn = slot_row // CAP
    target = 4 * ((gx + turn // 4) & 3) + ((gz + turn) & 3)
    heir = GROUP * target + seat
    lane = lax.broadcasted_iota(jnp.int32, (1, ROWS), 1)
    first = count(point(lane * ROWS + heir) < group_first, 1)
    place = first + (slot_row & (CAP - 1))
    level = jnp.where(place < ROWS, point(place * ROWS + heir), jnp.int32(1 << 30))
    lower = lax.broadcasted_iota(jnp.int32, (ROWS, ROWS), 0) <= lax.broadcasted_iota(
        jnp.int32, (ROWS, ROWS), 1
    )
    mine = group_tickets[...]
    inner = jnp.dot(
        mine.astype(jnp.float32).astype(jnp.bfloat16),
        jnp.where(lower, 1.0, 0.0).astype(jnp.bfloat16),
        preferred_element_type=jnp.float32,
    )
    opened = before
    for d in range(GROUP):
        high = (opened + inner[d : d + 1, :]).astype(jnp.int32)
        low = high - mine[d : d + 1, :]
        onehot[:, d * ROWS : (d + 1) * ROWS] = jnp.where(
            (level >= low) & (level < high), 1.0, 0.0
        ).astype(jnp.bfloat16)
        opened = opened + inner[d : d + 1, ROWS - 1 : ROWS]

    wait_bytes(block(prev, 1), ring_recv.at[2])
    hand(prev, 1, 3)
    wait_bytes(block(after, 0), ring_recv.at[3])
    hand(after, 0, 4)
    wait_bytes(block(across, 0), ring_recv.at[4])
    hand(across, 0, 5)
    wait_bytes(block(across, 1), ring_recv.at[5])
    hand(across, 1, 6)
    wait_bytes(pool.at[pl.ds(0, 4 * ROWS)], pair_recv)

    home = pl.ds(pl.multiple_of(group * CAP, CAP), CAP)
    for part in range(4):
        chunk = slice(part * 4 * CAP, (part + 1) * 4 * CAP)
        outbox[chunk, :] = jnp.dot(
            onehot[chunk, :], pool[...], preferred_element_type=jnp.float32
        ).astype(jnp.bfloat16)
        for i in range(4 * part, 4 * part + 4):
            if i == 0:
                inbox[home, :] = outbox[0:CAP, :]
            else:
                remote(
                    outbox.at[pl.ds(i * CAP, CAP)], inbox.at[home], rows_send, rows_recv, rows[i - 1]
                ).start()

    loads[2].wait()

    def turn_over(i, carry):
        cols = pl.ds(pl.multiple_of(i * 256, 256), 256)
        for j in range(0, 1024, 256):
            cpl_t[cols, j : j + 256] = cpl[j : j + 256, cols].T
        return carry

    lax.fori_loop(0, 8, turn_over, 0)

    mark = lax.broadcasted_iota(jnp.int32, (1, GROUPS * CAP), 1)
    origin = mark // CAP
    opens = jnp.sum(
        jnp.where(device < GROUP * origin, totals, 0.0), axis=0, keepdims=True
    ).astype(jnp.int32)
    closes = jnp.sum(
        jnp.where(device < GROUP * origin + GROUP, totals, 0.0), axis=0, keepdims=True
    ).astype(jnp.int32)
    needs = point(device * ROWS + me)
    skipped = count(needs < opens, 0)
    chosen = (device - skipped == (mark & (CAP - 1))) & (needs >= opens) & (needs < closes)
    selector = jnp.where(chosen, 1.0, 0.0).astype(jnp.bfloat16)

    for copy in loads[3:]:
        copy.wait()
    wait_bytes(inbox.at[pl.ds(0, (GROUPS - 1) * CAP)], rows_recv)
    start = jnp.dot(selector, inbox[...], preferred_element_type=jnp.float32)
    vis[...] = start
    visb[...] = start.astype(jnp.bfloat16)

    def sweep(s, carry):
        for n in range(0, 2048, 256):
            cols = slice(n, n + 256)
            pre = jnp.dot(visb[...], cpl[:, cols], preferred_element_type=jnp.float32)
            field = pre + hb[:, cols] + nz[s, :, cols].astype(jnp.float32)
            hid[:, cols] = logistic(field).astype(jnp.bfloat16)
        for n in range(0, 1024, 256):
            cols = slice(n, n + 256)
            pre = jnp.dot(hid[...], cpl_t[:, cols], preferred_element_type=jnp.float32)
            new = 0.5 * vis[:, cols] + 0.5 * logistic(pre + vb[:, cols])
            vis[:, cols] = new
            visb[:, cols] = new.astype(jnp.bfloat16)
        return carry

    lax.fori_loop(0, SWEEPS, sweep, 0)
    result = pltpu.make_async_copy(vis, visible_ref, out_sem)
    result.start()

    energy = jnp.sum(vis[...] * vb[...], axis=1, keepdims=True)
    for n in range(0, 2048, 256):
        cols = slice(n, n + 256)
        act = jnp.dot(visb[...], cpl[:, cols], preferred_element_type=jnp.float32) + hb[:, cols]
        soft = jnp.maximum(act, 0.0) + jnp.log(1.0 + jnp.exp(-jnp.abs(act)))
        energy = energy + jnp.sum(soft, axis=1, keepdims=True)
    beta_step = 204.8 / 2048
    log_weight = beta_step * energy
    diagonal = device == lane
    flat = jnp.sum(jnp.where(diagonal, log_weight, 0.0), axis=0, keepdims=True)

    def packed(top, total):
        return jnp.where(lane < ROWS // 2, top, total)

    def merged(ref):
        both = ref[...]
        sums = pltpu.roll(both, ROWS // 2, 1)
        head = lax.broadcasted_iota(jnp.int32, both.shape, 1) < ROWS // 2
        top = jnp.max(jnp.where(head, both, -jnp.inf), axis=(0, 1), keepdims=True)
        one = lax.broadcasted_iota(jnp.int32, both.shape, 1) == 0
        scaled = jnp.where(one, sums * jnp.exp(jnp.where(one, both, top) - top), 0.0)
        return top, jnp.sum(scaled, axis=(0, 1), keepdims=True)

    top = jnp.max(flat, axis=1, keepdims=True)
    total = jnp.sum(jnp.exp(flat - top), axis=1, keepdims=True)
    own_stat[0:1, :] = packed(top, total)
    group_stats[pl.ds(seat, 1), :] = packed(top, total)
    for t in mates:
        remote(
            own_stat.at[pl.ds(0, 1)],
            group_stats.at[pl.ds(seat, 1)],
            stat_sems.at[0],
            stat_sems.at[1],
            t,
        ).start()
    wait_bytes(group_stats.at[pl.ds(0, GROUP - 1)], stat_sems.at[1])
    top, total = merged(group_stats)
    own_stat[8:9, :] = packed(top, total)
    all_stats[pl.ds(group, 1), :] = packed(top, total)
    for t in rows:
        remote(
            own_stat.at[pl.ds(8, 1)],
            all_stats.at[pl.ds(group, 1)],
            stat_sems.at[2],
            stat_sems.at[3],
            t,
        ).start()

    for copy in sends:
        copy.wait_send()
    wait_bytes(group_tickets.at[pl.ds(0, GROUP - 1)], tick_sems.at[0])
    wait_bytes(all_tickets.at[pl.ds(0, (GROUPS - 1) * GROUP)], tick_sems.at[2])
    wait_bytes(outbox.at[pl.ds(CAP, (GROUPS - 1) * CAP)], rows_send)
    wait_bytes(group_stats.at[pl.ds(0, GROUP - 1)], stat_sems.at[0])

    wait_bytes(all_stats.at[pl.ds(0, GROUPS - 1)], stat_sems.at[3])
    top, total = merged(all_stats)
    weights_ref[...] = jnp.exp(flat - top) * (CHAINS / total)
    ratio_ref[...] = top + jnp.log(total) - jnp.log(jnp.full((1, 1), CHAINS, jnp.float32))
    wait_bytes(all_stats.at[pl.ds(0, GROUPS - 1)], stat_sems.at[2])
    result.wait()


def per_device(states, coupling, vis_bias, hid_bias, noise, tickets, offset):
    f32, b16, i32 = jnp.float32, jnp.bfloat16, jnp.int32
    anywhere = pl.BlockSpec(memory_space=pl.ANY)
    dma = pltpu.SemaphoreType.DMA
    visible, weights, ratio = pl.pallas_call(
        step_kernel,
        out_shape=(
            jax.ShapeDtypeStruct((ROWS, 1024), f32),
            jax.ShapeDtypeStruct((1, ROWS), f32),
            jax.ShapeDtypeStruct((1, 1), f32),
        ),
        in_specs=[anywhere] * 6 + [pl.BlockSpec(memory_space=pltpu.SMEM)],
        out_specs=(
            anywhere,
            pl.BlockSpec(memory_space=pltpu.VMEM),
            pl.BlockSpec(memory_space=pltpu.VMEM),
        ),
        scratch_shapes=[
            pltpu.VMEM((1, ROWS), i32),
            pltpu.VMEM((GROUP, ROWS), i32),
            pltpu.VMEM((ROWS, ROWS), i32),
            pltpu.VMEM((ROWS, 1024), f32),
            pltpu.VMEM((GROUP * ROWS, 1024), b16),
            pltpu.VMEM((GROUPS * CAP, GROUP * ROWS), b16),
            pltpu.VMEM((GROUPS * CAP, 1024), b16),
            pltpu.VMEM((GROUPS * CAP, 1024), b16),
            pltpu.VMEM((1024, 2048), b16),
            pltpu.VMEM((2048, 1024), b16),
            pltpu.VMEM((SWEEPS, ROWS, 2048), b16),
            pltpu.VMEM((1, 2048), f32),
            pltpu.VMEM((1, 1024), f32),
            pltpu.VMEM((ROWS, 2048), b16),
            pltpu.VMEM((ROWS, 1024), b16),
            pltpu.VMEM((16, ROWS), f32),
            pltpu.VMEM((GROUP, ROWS), f32),
            pltpu.VMEM((GROUPS, ROWS), f32),
            dma((6,)),
            dma((4,)),
            dma((6,)),
            dma((6,)),
            dma((7,)),
            dma(()),
            dma(()),
            dma(()),
            dma((4,)),
            dma(()),
        ],
        compiler_params=pltpu.CompilerParams(collective_id=1, has_side_effects=True),
    )(
        states,
        coupling,
        vis_bias.reshape(1, 1024),
        hid_bias.reshape(1, 2048),
        noise,
        tickets.reshape(1, ROWS),
        offset,
    )
    return visible, weights.reshape(ROWS), ratio.reshape(())


def solution(mesh):
    both = ("grp", "rep")
    return jax.shard_map(
        per_device,
        mesh=mesh,
        in_specs=(P(both, None), P(), P(), P(), P(None, both, None), P(both), P()),
        out_specs=(P(both, None), P(both), P()),
        check_vma=False,
    )
```

time: 148 us -> 60.2 us (0.41)
  Pallas kernels: 0 us -> 53.9 us
  blocking collectives: 39.7 us -> 0 us
  matrix products: 29.4 us -> 0 us
  waiting for transfers between devices: 28.3 us -> 0 us
  other arithmetic: 17.6 us -> 0 us
  starting transfers between devices: 16.5 us -> 0 us
  local copies, waits for them, and re-layouts: 8.93 us -> 2.99 us
  between operations: 7.31 us -> 3.05 us
    pallas_call x0 -> x1, Pallas kernels: none -> 53.9 us  [per_device(): pl.pallas_call(step_kernel, out_shape=(jax.ShapeDtypeStruct((ROWS, 1024),...]
    all_to_all x5 -> x0, blocking collectives: 39.7 us -> none  [copy_for_each(): lax.all_to_all(jnp.broadcast_to(array[None], (length, *array.shape)), axi...]
    dot_general x6 -> x0, matrix products: 29.4 us -> none  [the longest x4 25.3 us: per_device(): lax.dot_general(hidden, coupling, (((1,), (1,)), ((), ())), preferred_ele...]
    all_to_all x2 -> x0, waiting for transfers between devices: 28.3 us -> none  [the longest x1 20.4 us: side_by_side(): lax.all_to_all(both, axis, split_axis=split_dim, concat_axis=concat_dim,...]
    all_to_all x2 -> x0, starting transfers between devices: 16.5 us -> none  [the longest x1 11.5 us: copy_for_each(): lax.all_to_all(jnp.broadcast_to(array[None], (length, *array.shape)), axi...]
    reduce_sum x7 -> x0, other arithmetic: 5.39 us -> none  [the longest x1 1.35 us: per_device(): own_total = jnp.sum(tickets)]
    broadcast_in_dim x6 -> x0, local copies, waits for them, and re-layouts: 3.9 us -> none  [copy_for_each(): jnp.broadcast_to(array[None], (length, *array.shape))]
    unnamed x10 -> x2, local copies, waits for them, and re-layouts: 0.03 us -> 2.99 us
  transfers between devices with their start and end apart: 2 -> 0, of which waited for: 2 -> 0; matrix products, arithmetic and copies ran while one was open for 1% -> 0% of each run, Pallas kernels for 0% -> 0%
where the time goes in v1:
time: 60.2 us; the launch traced here: 60 us
  Pallas kernels  53.9 us (90%)
  between operations  3.05 us (5%)
  local copies, waits for them, and re-layouts  2.99 us (5%)
    pallas_call x1, Pallas kernels, per_device(): pl.pallas_call(step_kernel, out_shape=(jax.ShapeDtypeStruct((ROWS, 1024),...  53.9 us
    unnamed x2, local copies, waits for them, and re-layouts  2.99 us

profile of v1, /device:TPU:0, one launch (start us, length us, event | category | flops | bytes accessed | tf_op | source)
XLA Modules:
  0.0 60.0 jit_solution(3193838685607741752)
XLA Ops:
  1.3 53.9 %shard_map.94 = (f32[128,1024]{1,0:T(8,128)}, f32[1,128]{1,0:T(1,128)}, f32[1,1]{1,0:T(1,128)}) custom-call(f32[128,1024]{1,0:T(8,128)} %states_ref.1, bf16[1024,2048]{1,0:T(8,128)(2,1)} %coupling_ref.1, f32[1,1024]{1,0:T(1,128)} %bitcast.6, f32[1,2048]{1,0:T(1,128)} %bitcast.5, bf16[4,128,2048]{2,1,0:T(8,128)(2,1)} %noise_ref.1, s32[1,128]{1,0:T(1,128)} %bitcast.7, ...), custom_call_target="tpu_custom_call" | custom-call | tf_op jit(solution)/shard_map/pallas_call | solution.py:360
  55.2 1.9 %copy.14 = f32[128,1024]{1,0:T(8,128)} copy(f32[128,1024]{1,0:T(8,128)} %get-tuple-element.12) | data formatting | bytes 1048576
  57.1 1.1 %copy.15 = f32[128]{0:T(128)} copy(f32[128]{0:T(128)} %bitcast.8) | data formatting | bytes 1024

commit v2 on v1

--- a/solution.py
+++ b/solution.py
@@ -1,3 +1,5 @@
+import functools
+
 import jax
 import jax.numpy as jnp
 from jax import lax
@@ -8,9 +10,9 @@
 MESH = pl.DeviceIdType.MESH
 SWEEPS = 4
 ROWS = 128
-GROUP = 8
-GROUPS = 16
-CAP = 32
+GROUP = 4
+GROUPS = 32
+NARROW, WIDE = 8, 16
 SHIFT = 14
 CHAINS = 1 << SHIFT
 
@@ -39,16 +41,19 @@
 
 
 def step_kernel(
+    cap,
     states_ref,
     coupling_ref,
     vis_bias_ref,
     hid_bias_ref,
     noise_ref,
     tickets_ref,
-    offset_ref,
+    offset_hbm,
     visible_ref,
     weights_ref,
     ratio_ref,
+    spill_ref,
+    offset_ref,
     own_tickets,
     group_tickets,
     all_tickets,
@@ -83,17 +88,22 @@
     seat = lax.rem(me, GROUP)
     line = lax.rem(me // 2, 4)
     group = me // GROUP
-    gx, gz = group // 4, lax.rem(group, 4)
+    gx, gz = me // 32, lax.rem(me // 8, 4)
     base = me - seat
     sibling = me + 1 - 2 * core
-    up = base + 2 * lax.rem(line + 1, 4) + core
-    down = base + 2 * lax.rem(line + 3, 4) + core
+    partner = base + lax.rem(seat + 2, GROUP)
     mates = [base + lax.rem(seat + i, GROUP) for i in range(1, GROUP)]
 
-    def plane(i):
-        return 4 * lax.rem(gx + i // 4, 4) + lax.rem(gz + i % 4, 4)
-
-    rows = [GROUP * plane(i) + seat for i in range(1, GROUPS)]
+    def away(i):
+        x = lax.rem(gx + i // 8, 4)
+        z = lax.rem(gz + i // 2 % 4, 4)
+        return 8 * (4 * x + z) + 2 * (line + i % 2 * (3 - 2 * line)) + core
+
+    def hops(i):
+        return (0, 1, 2, 1)[i // 8] + (0, 1, 2, 1)[i // 2 % 4] + i % 2
+
+    order = sorted(range(1, GROUPS), key=hops, reverse=True)
+    rows = [away(i) for i in order]
 
     barrier = pltpu.get_barrier_semaphore()
     for t in mates + rows:
@@ -109,6 +119,7 @@
                 (noise_ref, nz),
                 (hid_bias_ref, hb),
                 (vis_bias_ref, vb),
+                (offset_hbm, offset_ref),
             )
         )
     ]
@@ -133,32 +144,15 @@
         ).start()
     sends = []
 
-    def ring(owner, half, to_up, slot):
-        copy = remote(
-            block(owner, half),
-            block(owner, half),
-            ring_send.at[slot],
-            ring_recv.at[slot],
-            up if to_up else down,
-        )
+    def pass_on(owner, half, send, recv, t):
+        copy = remote(block(owner, half), block(owner, half), send, recv, t)
         copy.start()
         sends.append(copy)
 
-    def hand(owner, half, slot):
-        copy = remote(
-            block(owner, half), block(owner, half), pair_send.at[slot], pair_recv, sibling
-        )
-        copy.start()
-        sends.append(copy)
-
-    prev = lax.rem(seat + 6, GROUP)
-    after = lax.rem(seat + 2, GROUP)
-    across = lax.rem(seat + 4, GROUP)
-    ring(seat, 0, True, 0)
-    ring(seat, 1, False, 1)
-    ring(seat, 1, True, 2)
-    ring(seat, 0, False, 3)
-    hand(seat, None, 0)
+    opposite = lax.rem(seat + 2, GROUP)
+    pass_on(seat, 0, ring_send.at[0], ring_recv.at[0], partner)
+    pass_on(seat, 1, ring_send.at[1], ring_recv.at[1], partner)
+    pass_on(seat, None, pair_send.at[0], pair_recv, sibling)
 
     wait_bytes(group_tickets.at[pl.ds(0, GROUP - 1)], tick_sems.at[1])
     my_rows = pl.ds(pl.multiple_of(base, GROUP), GROUP)
@@ -168,37 +162,37 @@
             group_tickets, all_tickets.at[my_rows], tick_sems.at[2], tick_sems.at[3], t
         ).start()
 
-    wait_bytes(block(prev, 0), ring_recv.at[0])
-    ring(prev, 0, True, 4)
-    hand(prev, 0, 1)
-    wait_bytes(block(after, 1), ring_recv.at[1])
-    ring(after, 1, False, 5)
-    hand(after, 1, 2)
-
+    loads[6].wait()
     wait_bytes(all_tickets.at[pl.ds(0, (GROUPS - 1) * GROUP)], tick_sems.at[3])
+    device = lax.broadcasted_iota(jnp.int32, (ROWS, 1), 0)
+    lane = lax.broadcasted_iota(jnp.int32, (1, ROWS), 1)
     everything = all_tickets[...].astype(jnp.float32)
     totals = jnp.sum(everything, axis=1, keepdims=True)
     grand = jnp.sum(totals, axis=0, keepdims=True).astype(jnp.int32)
     z_high, z_low = grand >> SHIFT, grand & (CHAINS - 1)
     jitter = offset_ref[0]
 
+    lines = jnp.sum(
+        jnp.where(device // GROUP == lane // GROUP, totals, 0.0), axis=0, keepdims=True
+    )
+    most = jnp.max(lines, axis=1, keepdims=True).astype(jnp.int32)
+    spill_ref[...] = jnp.where(most * ROWS <= cap * grand, 0, 1)
+
     def point(k):
         return k * z_high + ((k * z_low + jitter) >> SHIFT)
 
     def count(mask, axis):
         return jnp.sum(jnp.where(mask, 1.0, 0.0), axis=axis, keepdims=True).astype(jnp.int32)
 
-    device = lax.broadcasted_iota(jnp.int32, (ROWS, 1), 0)
     before = jnp.sum(jnp.where(device < base, totals, 0.0), axis=0, keepdims=True)
     group_first = before.astype(jnp.int32)
 
-    slot_row = lax.broadcasted_iota(jnp.int32, (GROUPS * CAP, 1), 0)
-    turn = slot_row // CAP
-    target = 4 * ((gx + turn // 4) & 3) + ((gz + turn) & 3)
-    heir = GROUP * target + seat
-    lane = lax.broadcasted_iota(jnp.int32, (1, ROWS), 1)
+    slot_row = lax.broadcasted_iota(jnp.int32, (GROUPS * cap, 1), 0)
+    turn = slot_row // cap
+    spot = 4 * ((gx + turn // 8) & 3) + ((gz + turn // 2) & 3)
+    heir = 8 * spot + 2 * (line + (turn & 1) * (3 - 2 * line)) + core
     first = count(point(lane * ROWS + heir) < group_first, 1)
-    place = first + (slot_row & (CAP - 1))
+    place = first + (slot_row & (cap - 1))
     level = jnp.where(place < ROWS, point(place * ROWS + heir), jnp.int32(1 << 30))
     lower = lax.broadcasted_iota(jnp.int32, (ROWS, ROWS), 0) <= lax.broadcasted_iota(
         jnp.int32, (ROWS, ROWS), 1
@@ -218,29 +212,22 @@
         ).astype(jnp.bfloat16)
         opened = opened + inner[d : d + 1, ROWS - 1 : ROWS]
 
-    wait_bytes(block(prev, 1), ring_recv.at[2])
-    hand(prev, 1, 3)
-    wait_bytes(block(after, 0), ring_recv.at[3])
-    hand(after, 0, 4)
-    wait_bytes(block(across, 0), ring_recv.at[4])
-    hand(across, 0, 5)
-    wait_bytes(block(across, 1), ring_recv.at[5])
-    hand(across, 1, 6)
-    wait_bytes(pool.at[pl.ds(0, 4 * ROWS)], pair_recv)
-
-    home = pl.ds(pl.multiple_of(group * CAP, CAP), CAP)
-    for part in range(4):
-        chunk = slice(part * 4 * CAP, (part + 1) * 4 * CAP)
-        outbox[chunk, :] = jnp.dot(
-            onehot[chunk, :], pool[...], preferred_element_type=jnp.float32
-        ).astype(jnp.bfloat16)
-        for i in range(4 * part, 4 * part + 4):
-            if i == 0:
-                inbox[home, :] = outbox[0:CAP, :]
-            else:
-                remote(
-                    outbox.at[pl.ds(i * CAP, CAP)], inbox.at[home], rows_send, rows_recv, rows[i - 1]
-                ).start()
+    for half in range(2):
+        wait_bytes(block(opposite, half), ring_recv.at[half])
+        pass_on(opposite, half, pair_send.at[1 + half], pair_recv, sibling)
+    wait_bytes(pool.at[pl.ds(0, 2 * ROWS)], pair_recv)
+
+    for part in range(0, GROUPS, ROWS // cap):
+        chunk = slice(part * cap, part * cap + ROWS)
+        picked = jnp.dot(onehot[chunk, :], pool[...], preferred_element_type=jnp.float32)
+        outbox[part : part + ROWS // cap] = picked.reshape(ROWS // cap, cap, 1024).astype(
+            jnp.bfloat16
+        )
+    inbox[pl.ds(group, 1)] = outbox[0:1]
+    for i, t in zip(order, rows):
+        remote(
+            outbox.at[pl.ds(i, 1)], inbox.at[pl.ds(group, 1)], rows_send, rows_recv, t
+        ).start()
 
     loads[2].wait()
 
@@ -252,8 +239,8 @@
 
     lax.fori_loop(0, 8, turn_over, 0)
 
-    mark = lax.broadcasted_iota(jnp.int32, (1, GROUPS * CAP), 1)
-    origin = mark // CAP
+    mark = lax.broadcasted_iota(jnp.int32, (1, GROUPS * cap), 1)
+    origin = mark // cap
     opens = jnp.sum(
         jnp.where(device < GROUP * origin, totals, 0.0), axis=0, keepdims=True
     ).astype(jnp.int32)
@@ -262,13 +249,14 @@
     ).astype(jnp.int32)
     needs = point(device * ROWS + me)
     skipped = count(needs < opens, 0)
-    chosen = (device - skipped == (mark & (CAP - 1))) & (needs >= opens) & (needs < closes)
+    chosen = (device - skipped == (mark & (cap - 1))) & (needs >= opens) & (needs < closes)
     selector = jnp.where(chosen, 1.0, 0.0).astype(jnp.bfloat16)
 
-    for copy in loads[3:]:
+    for copy in loads[3:6]:
         copy.wait()
-    wait_bytes(inbox.at[pl.ds(0, (GROUPS - 1) * CAP)], rows_recv)
-    start = jnp.dot(selector, inbox[...], preferred_element_type=jnp.float32)
+    wait_bytes(inbox.at[pl.ds(0, GROUPS - 1)], rows_recv)
+    arrived = inbox[...].astype(jnp.float32).reshape(GROUPS * cap, 1024).astype(jnp.bfloat16)
+    start = jnp.dot(selector, arrived, preferred_element_type=jnp.float32)
     vis[...] = start
     visb[...] = start.astype(jnp.bfloat16)
 
@@ -342,7 +330,7 @@
         copy.wait_send()
     wait_bytes(group_tickets.at[pl.ds(0, GROUP - 1)], tick_sems.at[0])
     wait_bytes(all_tickets.at[pl.ds(0, (GROUPS - 1) * GROUP)], tick_sems.at[2])
-    wait_bytes(outbox.at[pl.ds(CAP, (GROUPS - 1) * CAP)], rows_send)
+    wait_bytes(outbox.at[pl.ds(1, GROUPS - 1)], rows_send)
     wait_bytes(group_stats.at[pl.ds(0, GROUP - 1)], stat_sems.at[0])
 
     wait_bytes(all_stats.at[pl.ds(0, GROUPS - 1)], stat_sems.at[3])
@@ -353,32 +341,35 @@
     result.wait()
 
 
-def per_device(states, coupling, vis_bias, hid_bias, noise, tickets, offset):
+def run(cap, ident, *arrays):
     f32, b16, i32 = jnp.float32, jnp.bfloat16, jnp.int32
     anywhere = pl.BlockSpec(memory_space=pl.ANY)
     dma = pltpu.SemaphoreType.DMA
-    visible, weights, ratio = pl.pallas_call(
-        step_kernel,
+    return pl.pallas_call(
+        functools.partial(step_kernel, cap),
         out_shape=(
             jax.ShapeDtypeStruct((ROWS, 1024), f32),
             jax.ShapeDtypeStruct((1, ROWS), f32),
             jax.ShapeDtypeStruct((1, 1), f32),
+            jax.ShapeDtypeStruct((1, 1), i32),
         ),
-        in_specs=[anywhere] * 6 + [pl.BlockSpec(memory_space=pltpu.SMEM)],
+        in_specs=[anywhere] * 7,
         out_specs=(
             anywhere,
             pl.BlockSpec(memory_space=pltpu.VMEM),
             pl.BlockSpec(memory_space=pltpu.VMEM),
+            pl.BlockSpec(memory_space=pltpu.VMEM),
         ),
         scratch_shapes=[
+            pltpu.SMEM((1,), i32),
             pltpu.VMEM((1, ROWS), i32),
             pltpu.VMEM((GROUP, ROWS), i32),
             pltpu.VMEM((ROWS, ROWS), i32),
             pltpu.VMEM((ROWS, 1024), f32),
             pltpu.VMEM((GROUP * ROWS, 1024), b16),
-            pltpu.VMEM((GROUPS * CAP, GROUP * ROWS), b16),
-            pltpu.VMEM((GROUPS * CAP, 1024), b16),
-            pltpu.VMEM((GROUPS * CAP, 1024), b16),
+            pltpu.VMEM((GROUPS * cap, GROUP * ROWS), b16),
+            pltpu.VMEM((GROUPS, cap, 1024), b16),
+            pltpu.VMEM((GROUPS, cap, 1024), b16),
             pltpu.VMEM((1024, 2048), b16),
             pltpu.VMEM((2048, 1024), b16),
             pltpu.VMEM((SWEEPS, ROWS, 2048), b16),
@@ -389,19 +380,23 @@
             pltpu.VMEM((16, ROWS), f32),
             pltpu.VMEM((GROUP, ROWS), f32),
             pltpu.VMEM((GROUPS, ROWS), f32),
-            dma((6,)),
+            dma((7,)),
             dma((4,)),
-            dma((6,)),
-            dma((6,)),
-            dma((7,)),
+            dma((2,)),
+            dma((2,)),
+            dma((3,)),
             dma(()),
             dma(()),
             dma(()),
             dma((4,)),
             dma(()),
         ],
-        compiler_params=pltpu.CompilerParams(collective_id=1, has_side_effects=True),
-    )(
+        compiler_params=pltpu.CompilerParams(collective_id=ident, has_side_effects=True),
+    )(*arrays)
+
+
+def per_device(states, coupling, vis_bias, hid_bias, noise, tickets, offset):
+    arrays = (
         states,
         coupling,
         vis_bias.reshape(1, 1024),
@@ -409,6 +404,13 @@
         noise,
         tickets.reshape(1, ROWS),
         offset,
+    )
+    visible, weights, ratio, spill = run(NARROW, 1, *arrays)
+    visible, weights, ratio = lax.cond(
+        spill[0, 0] > 0,
+        lambda kept: tuple(run(WIDE, 2, *arrays)[:3]),
+        lambda kept: kept,
+        (visible, weights, ratio),
     )
     return visible, weights.reshape(ROWS), ratio.reshape(())
 

time: 60.2 us -> 48.3 us (0.80)
  Pallas kernels: 53.9 us -> 42.9 us
  local copies, waits for them, and re-layouts: 2.99 us -> 1.33 us
  between operations: 3.05 us -> 3.91 us
    pallas_call x1, Pallas kernels: 53.9 us -> 42.9 us  [run(): pl.pallas_call(functools.partial(step_kernel, cap), out_shape=(jax.ShapeD...]
    unnamed x2 -> x12, local copies, waits for them, and re-layouts: 2.99 us -> 1.33 us
where the time goes in v2:
time: 48.3 us; the launch traced here: 48.2 us
  Pallas kernels  42.9 us (89%)
  between operations  3.91 us (8%)
  local copies, waits for them, and re-layouts  1.33 us (3%)
    pallas_call x1, Pallas kernels, run(): pl.pallas_call(functools.partial(step_kernel, cap), out_shape=(jax.ShapeD...  42.9 us
    unnamed x12, local copies, waits for them, and re-layouts  1.33 us

profile of v2, /device:TPU:0, one launch (start us, length us, event | category | flops | bytes accessed | tf_op | source)
XLA Modules:
  0.0 48.2 jit_solution(926355626243195333)
XLA Ops:
  0.6 0.0 copy-start
  0.6 0.0 copy-start.1
  0.7 0.0 copy-start.4
  0.7 0.0 copy-start.2
  0.7 0.0 copy-start.3
  1.5 42.9 %shard_map.94 = (f32[128,1024]{1,0:T(8,128)S(1)}, f32[1,128]{1,0:T(1,128)S(1)}, f32[1,1]{1,0:T(1,128)}, s32[1,1]{1,0:T(1,128)}) custom-call(f32[128,1024]{1,0:T(8,128)} %states_ref.1, bf16[1024,2048]{1,0:T(8,128)(2,1)} %coupling_ref.1, f32[1,1024]{1,0:T(1,128)} %bitcast.8, f32[1,2048]{1,0:T(1,128)} %bitcast.6, bf16[4,128,2048]{2,1,0:T(8,128)(2,1)} %noise_ref.1, ...), custom_call_target="tpu_custom_call" | custom-call | tf_op jit(solution)/shard_map/pallas_call | solution.py:348
  45.1 0.0 copy-done
  45.1 0.0 copy-done.1
  45.1 0.0 copy-done.4
  45.1 0.0 copy-done.2
  45.1 0.0 copy-done.3
  45.1 0.8 %copy.20 = f32[128,1024]{1,0:T(8,128)} copy(f32[128,1024]{1,0:T(8,128)S(1)} %get-tuple-element.61) | data formatting | bytes 1048576
  45.9 0.5 %copy.21 = f32[128]{0:T(128)} copy(f32[128]{0:T(128)S(1)} %bitcast.12) | data formatting | bytes 1024
  (1 shorter events, 0.0 us)
Async XLA Ops:
  0.6 44.4 %copy-start = (bf16[4,128,2048]{2,1,0:T(8,128)(2,1)S(1)}, bf16[4,128,2048]{2,1,0:T(8,128)(2,1)}, u32[]{:S(2)}) copy-start(bf16[4,128,2048]{2,1,0:T(8,128)(2,1)} %noise_ref.1) | copy-start | bytes 6291460
  0.6 44.4 %copy-start.1 = (f32[128,1024]{1,0:T(8,128)S(1)}, f32[128,1024]{1,0:T(8,128)}, u32[]{:S(2)}) copy-start(f32[128,1024]{1,0:T(8,128)} %states_ref.1) | copy-start | bytes 1572868
  0.7 44.4 %copy-start.4 = (s32[128]{0:T(128)S(1)}, s32[128]{0:T(128)}, u32[]{:S(2)}) copy-start(s32[128]{0:T(128)} %param.14) | copy-start | bytes 1540
  0.7 44.4 %copy-start.2 = (f32[2048]{0:T(1024)S(1)}, f32[2048]{0:T(1024)}, u32[]{:S(2)}) copy-start(f32[2048]{0:T(1024)} %param.12) | copy-start | bytes 24580
  0.7 44.4 %copy-start.3 = (f32[1024]{0:T(1024)S(1)}, f32[1024]{0:T(1024)}, u32[]{:S(2)}) copy-start(f32[1024]{0:T(1024)} %param.11) | copy-start | bytes 12292

commit v3 on v2

--- a/solution.py
+++ b/solution.py
@@ -50,8 +50,7 @@
     tickets_ref,
     offset_hbm,
     visible_ref,
-    weights_ref,
-    ratio_ref,
+    small_ref,
     spill_ref,
     offset_ref,
     own_tickets,
@@ -170,13 +169,13 @@
     totals = jnp.sum(everything, axis=1, keepdims=True)
     grand = jnp.sum(totals, axis=0, keepdims=True).astype(jnp.int32)
     z_high, z_low = grand >> SHIFT, grand & (CHAINS - 1)
-    jitter = offset_ref[0]
+    jitter = offset_ref[...]
 
     lines = jnp.sum(
         jnp.where(device // GROUP == lane // GROUP, totals, 0.0), axis=0, keepdims=True
     )
     most = jnp.max(lines, axis=1, keepdims=True).astype(jnp.int32)
-    spill_ref[...] = jnp.where(most * ROWS <= cap * grand, 0, 1)
+    spill_ref[0, 0] = jnp.where(most * ROWS <= cap * grand, 0, 1)[0, 0]
 
     def point(k):
         return k * z_high + ((k * z_low + jitter) >> SHIFT)
@@ -274,7 +273,11 @@
             visb[:, cols] = new.astype(jnp.bfloat16)
         return carry
 
-    lax.fori_loop(0, SWEEPS, sweep, 0)
+    if cap == NARROW:
+        for s in range(SWEEPS):
+            sweep(s, 0)
+    else:
+        lax.fori_loop(0, SWEEPS, sweep, 0)
     result = pltpu.make_async_copy(vis, visible_ref, out_sem)
     result.start()
 
@@ -335,10 +338,25 @@
 
     wait_bytes(all_stats.at[pl.ds(0, GROUPS - 1)], stat_sems.at[3])
     top, total = merged(all_stats)
-    weights_ref[...] = jnp.exp(flat - top) * (CHAINS / total)
-    ratio_ref[...] = top + jnp.log(total) - jnp.log(jnp.full((1, 1), CHAINS, jnp.float32))
+    small_ref[:, :ROWS] = jnp.exp(flat - top) * (CHAINS / total)
+    ratio = top + jnp.log(total) - jnp.log(jnp.full((1, 1), CHAINS, jnp.float32))
+    small_ref[:, ROWS:] = jnp.broadcast_to(ratio, (1, ROWS))
     wait_bytes(all_stats.at[pl.ds(0, GROUPS - 1)], stat_sems.at[2])
     result.wait()
+
+
+def finish_kernel(visible, small, visible_out, weights_out, ratio_out, ratio, sems):
+    ratio[...] = small[:, ROWS : ROWS + 1]
+    copies = [
+        pltpu.make_async_copy(src, dst, sems.at[i])
+        for i, (src, dst) in enumerate(
+            ((visible, visible_out), (small.at[:, pl.ds(0, ROWS)], weights_out), (ratio, ratio_out))
+        )
+    ]
+    for copy in copies:
+        copy.start()
+    for copy in copies:
+        copy.wait()
 
 
 def run(cap, ident, *arrays):
@@ -349,19 +367,17 @@
         functools.partial(step_kernel, cap),
         out_shape=(
             jax.ShapeDtypeStruct((ROWS, 1024), f32),
-            jax.ShapeDtypeStruct((1, ROWS), f32),
-            jax.ShapeDtypeStruct((1, 1), f32),
+            jax.ShapeDtypeStruct((1, 2 * ROWS), f32),
             jax.ShapeDtypeStruct((1, 1), i32),
         ),
         in_specs=[anywhere] * 7,
         out_specs=(
             anywhere,
             pl.BlockSpec(memory_space=pltpu.VMEM),
-            pl.BlockSpec(memory_space=pltpu.VMEM),
-            pl.BlockSpec(memory_space=pltpu.VMEM),
+            pl.BlockSpec(memory_space=pltpu.SMEM),
         ),
         scratch_shapes=[
-            pltpu.SMEM((1,), i32),
+            pltpu.VMEM((1, 1), i32),
             pltpu.VMEM((1, ROWS), i32),
             pltpu.VMEM((GROUP, ROWS), i32),
             pltpu.VMEM((ROWS, ROWS), i32),
@@ -403,15 +419,26 @@
         hid_bias.reshape(1, 2048),
         noise,
         tickets.reshape(1, ROWS),
-        offset,
-    )
-    visible, weights, ratio, spill = run(NARROW, 1, *arrays)
-    visible, weights, ratio = lax.cond(
+        offset.reshape(1, 1),
+    )
+    visible, small, spill = run(NARROW, 1, *arrays)
+    visible, small = lax.cond(
         spill[0, 0] > 0,
-        lambda kept: tuple(run(WIDE, 2, *arrays)[:3]),
+        lambda kept: tuple(run(WIDE, 2, *arrays)[:2]),
         lambda kept: kept,
-        (visible, weights, ratio),
-    )
+        (visible, small),
+    )
+    inside = pl.BlockSpec(memory_space=pltpu.VMEM)
+    outside = pl.BlockSpec(memory_space=pl.ANY)
+    visible, weights, ratio = pl.pallas_call(
+        finish_kernel,
+        out_shape=tuple(
+            jax.ShapeDtypeStruct(shape, jnp.float32) for shape in ((ROWS, 1024), (1, ROWS), (1, 1))
+        ),
+        in_specs=[inside] * 2,
+        out_specs=[outside] * 3,
+        scratch_shapes=[pltpu.VMEM((1, 1), jnp.float32), pltpu.SemaphoreType.DMA((3,))],
+    )(visible, small)
     return visible, weights.reshape(ROWS), ratio.reshape(())
 
 

time: 48.3 us -> 45.5 us (0.942)
  between operations: 3.91 us -> 2.32 us
  local copies, waits for them, and re-layouts: 1.33 us -> 0.02 us
    unnamed x12 -> x10, local copies, waits for them, and re-layouts: 1.33 us -> 0.02 us
    pallas_call x1, Pallas kernels: 42.9 us -> 42 us  [run(): pl.pallas_call(functools.partial(step_kernel, cap), out_shape=(jax.ShapeD...]
    pallas_call x0 -> x1, Pallas kernels: none -> 0.83 us  [per_device(): pl.pallas_call(finish_kernel, out_shape=tuple((jax.ShapeDtypeStruct(shape...]
where the time goes in v3:
time: 45.5 us; the launch traced here: 45.3 us
  Pallas kernels  42.8 us (94%)
  between operations  2.32 us (5%)
    pallas_call x1, Pallas kernels, run(): pl.pallas_call(functools.partial(step_kernel, cap), out_shape=(jax.ShapeD...  42 us

profile of v3, /device:TPU:0, one launch (start us, length us, event | category | flops | bytes accessed | tf_op | source)
XLA Modules:
  0.0 45.3 jit_solution(13055189893800585635)
XLA Ops:
  0.6 0.0 copy-start
  0.6 0.0 copy-start.1
  0.7 0.0 copy-start.4
  0.7 0.0 copy-start.2
  0.7 0.0 copy-start.3
  1.5 42.0 %shard_map.94 = (f32[128,1024]{1,0:T(8,128)S(1)}, f32[1,256]{1,0:T(1,128)S(1)}, s32[1,1]{1,0:T(1,128)}) custom-call(f32[128,1024]{1,0:T(8,128)} %states_ref.1, bf16[1024,2048]{1,0:T(8,128)(2,1)} %coupling_ref.1, f32[1,1024]{1,0:T(1,128)} %bitcast.10, f32[1,2048]{1,0:T(1,128)} %bitcast.8, bf16[4,128,2048]{2,1,0:T(8,128)(2,1)} %noise_ref.1, ...), custom_call_target="tpu_custom_call" | custom-call | tf_op jit(solution)/shard_map/pallas_call | solution.py:366
  44.1 0.0 copy-done
  44.1 0.0 copy-done.1
  44.1 0.0 copy-done.4
  44.1 0.0 copy-done.2
  44.1 0.0 copy-done.3
  44.1 0.2 conditional.1
  44.3 0.8 %shard_map.95 = (f32[128,1024]{1,0:T(8,128)}, f32[1,128]{1,0:T(1,128)}, f32[1,1]{1,0:T(1,128)}) custom-call(f32[128,1024]{1,0:T(8,128)S(1)} %get-tuple-element.41.visible, f32[1,256]{1,0:T(1,128)S(1)} %get-tuple-element.42.small), custom_call_target="tpu_custom_call" | custom-call | tf_op jit(solution)/shard_map/pallas_call | solution.py:433
Async XLA Ops:
  0.6 43.5 %copy-start = (bf16[4,128,2048]{2,1,0:T(8,128)(2,1)S(1)}, bf16[4,128,2048]{2,1,0:T(8,128)(2,1)}, u32[]{:S(2)}) copy-start(bf16[4,128,2048]{2,1,0:T(8,128)(2,1)} %noise_ref.1) | copy-start | bytes 6291460
  0.6 43.5 %copy-start.1 = (f32[128,1024]{1,0:T(8,128)S(1)}, f32[128,1024]{1,0:T(8,128)}, u32[]{:S(2)}) copy-start(f32[128,1024]{1,0:T(8,128)} %states_ref.1) | copy-start | bytes 1572868
  0.7 43.5 %copy-start.4 = (s32[128]{0:T(128)S(1)}, s32[128]{0:T(128)}, u32[]{:S(2)}) copy-start(s32[128]{0:T(128)} %param.14) | copy-start | bytes 1540
  0.7 43.5 %copy-start.2 = (f32[2048]{0:T(1024)S(1)}, f32[2048]{0:T(1024)}, u32[]{:S(2)}) copy-start(f32[2048]{0:T(1024)} %param.12) | copy-start | bytes 24580
  0.7 43.5 %copy-start.3 = (f32[1024]{0:T(1024)S(1)}, f32[1024]{0:T(1024)}, u32[]{:S(2)}) copy-start(f32[1024]{0:T(1024)} %param.11) | copy-start | bytes 12292

commit v4 on v3

--- a/solution.py
+++ b/solution.py
@@ -69,7 +69,6 @@
     hid,
     visb,
     own_stat,
-    group_stats,
     all_stats,
     load_sems,
     tick_sems,
@@ -104,6 +103,18 @@
     order = sorted(range(1, GROUPS), key=hops, reverse=True)
     rows = [away(i) for i in order]
 
+    def everyone():
+        far = (0, 1, 2, 1)
+        steps = [
+            (x, z, y, c) for x in range(4) for z in range(4) for y in range(4) for c in range(2)
+        ][1:]
+        steps.sort(key=lambda d: (-far[d[0]] - far[d[1]] - far[d[2]], -d[3]))
+        xs = [16 * lax.rem(gx + i, 4) for i in range(4)]
+        zs = [4 * lax.rem(gz + i, 4) for i in range(4)]
+        ys = [lax.rem(line + i, 4) for i in range(4)]
+        cs = [core, 1 - core]
+        return [(xs[x] + zs[z] + ys[y], cs[c]) for x, z, y, c in steps]
+
     barrier = pltpu.get_barrier_semaphore()
     for t in mates + rows:
         pl.semaphore_signal(barrier, inc=1, device_id=where_is(t), device_id_type=MESH)
@@ -306,27 +317,16 @@
 
     top = jnp.max(flat, axis=1, keepdims=True)
     total = jnp.sum(jnp.exp(flat - top), axis=1, keepdims=True)
-    own_stat[0:1, :] = packed(top, total)
-    group_stats[pl.ds(seat, 1), :] = packed(top, total)
-    for t in mates:
-        remote(
-            own_stat.at[pl.ds(0, 1)],
-            group_stats.at[pl.ds(seat, 1)],
-            stat_sems.at[0],
-            stat_sems.at[1],
-            t,
-        ).start()
-    wait_bytes(group_stats.at[pl.ds(0, GROUP - 1)], stat_sems.at[1])
-    top, total = merged(group_stats)
-    own_stat[8:9, :] = packed(top, total)
-    all_stats[pl.ds(group, 1), :] = packed(top, total)
-    for t in rows:
-        remote(
-            own_stat.at[pl.ds(8, 1)],
-            all_stats.at[pl.ds(group, 1)],
-            stat_sems.at[2],
-            stat_sems.at[3],
-            t,
+    own_stat[...] = packed(top, total)
+    all_stats[pl.ds(me, 1), :] = packed(top, total)
+    for t in everyone():
+        pltpu.make_async_remote_copy(
+            src_ref=own_stat,
+            dst_ref=all_stats.at[pl.ds(me, 1)],
+            send_sem=stat_sems.at[0],
+            recv_sem=stat_sems.at[1],
+            device_id=t,
+            device_id_type=MESH,
         ).start()
 
     for copy in sends:
@@ -334,14 +334,13 @@
     wait_bytes(group_tickets.at[pl.ds(0, GROUP - 1)], tick_sems.at[0])
     wait_bytes(all_tickets.at[pl.ds(0, (GROUPS - 1) * GROUP)], tick_sems.at[2])
     wait_bytes(outbox.at[pl.ds(1, GROUPS - 1)], rows_send)
-    wait_bytes(group_stats.at[pl.ds(0, GROUP - 1)], stat_sems.at[0])
-
-    wait_bytes(all_stats.at[pl.ds(0, GROUPS - 1)], stat_sems.at[3])
+
+    wait_bytes(all_stats.at[pl.ds(0, ROWS - 1)], stat_sems.at[1])
     top, total = merged(all_stats)
     small_ref[:, :ROWS] = jnp.exp(flat - top) * (CHAINS / total)
     ratio = top + jnp.log(total) - jnp.log(jnp.full((1, 1), CHAINS, jnp.float32))
     small_ref[:, ROWS:] = jnp.broadcast_to(ratio, (1, ROWS))
-    wait_bytes(all_stats.at[pl.ds(0, GROUPS - 1)], stat_sems.at[2])
+    wait_bytes(all_stats.at[pl.ds(0, ROWS - 1)], stat_sems.at[0])
     result.wait()
 
 
@@ -393,9 +392,8 @@
             pltpu.VMEM((1, 1024), f32),
             pltpu.VMEM((ROWS, 2048), b16),
             pltpu.VMEM((ROWS, 1024), b16),
-            pltpu.VMEM((16, ROWS), f32),
-            pltpu.VMEM((GROUP, ROWS), f32),
-            pltpu.VMEM((GROUPS, ROWS), f32),
+            pltpu.VMEM((1, ROWS), f32),
+            pltpu.VMEM((ROWS, ROWS), f32),
             dma((7,)),
             dma((4,)),
             dma((2,)),
@@ -404,7 +402,7 @@
             dma(()),
             dma(()),
             dma(()),
-            dma((4,)),
+            dma((2,)),
             dma(()),
         ],
         compiler_params=pltpu.CompilerParams(collective_id=ident, has_side_effects=True),

time: 45.5 us -> 43.8 us (0.963); the launches traced: 45.3 us -> 43.1 us
  Pallas kernels: 42.8 us -> 40.5 us
    pallas_call x1, Pallas kernels: 42 us -> 39.7 us  [run(): pl.pallas_call(functools.partial(step_kernel, cap), out_shape=(jax.ShapeD...]
where the time goes in v4:
time: 43.8 us; the launch traced here: 43.1 us
  Pallas kernels  40.5 us (92%)
  between operations  2.32 us (5%)
    pallas_call x1, Pallas kernels, run(): pl.pallas_call(functools.partial(step_kernel, cap), out_shape=(jax.ShapeD...  39.7 us

profile of v4, /device:TPU:0, one launch (start us, length us, event | category | flops | bytes accessed | tf_op | source)
XLA Modules:
  0.0 43.1 jit_solution(9006867339468063875)
XLA Ops:
  0.6 0.0 copy-start
  0.6 0.0 copy-start.1
  0.7 0.0 copy-start.4
  0.7 0.0 copy-start.2
  0.7 0.0 copy-start.3
  1.5 39.7 %shard_map.94 = (f32[128,1024]{1,0:T(8,128)S(1)}, f32[1,256]{1,0:T(1,128)S(1)}, s32[1,1]{1,0:T(1,128)}) custom-call(f32[128,1024]{1,0:T(8,128)} %states_ref.1, bf16[1024,2048]{1,0:T(8,128)(2,1)} %coupling_ref.1, f32[1,1024]{1,0:T(1,128)} %bitcast.10, f32[1,2048]{1,0:T(1,128)} %bitcast.8, bf16[4,128,2048]{2,1,0:T(8,128)(2,1)} %noise_ref.1, ...), custom_call_target="tpu_custom_call" | custom-call | tf_op jit(solution)/shard_map/pallas_call | solution.py:365
  41.8 0.0 copy-done
  41.8 0.0 copy-done.1
  41.8 0.0 copy-done.4
  41.9 0.0 copy-done.2
  41.9 0.0 copy-done.3
  41.9 0.2 conditional.1
  42.1 0.8 %shard_map.95 = (f32[128,1024]{1,0:T(8,128)}, f32[1,128]{1,0:T(1,128)}, f32[1,1]{1,0:T(1,128)}) custom-call(f32[128,1024]{1,0:T(8,128)S(1)} %get-tuple-element.41.visible, f32[1,256]{1,0:T(1,128)S(1)} %get-tuple-element.42.small), custom_call_target="tpu_custom_call" | custom-call | tf_op jit(solution)/shard_map/pallas_call | solution.py:431
Async XLA Ops:
  0.6 41.2 %copy-start = (bf16[4,128,2048]{2,1,0:T(8,128)(2,1)S(1)}, bf16[4,128,2048]{2,1,0:T(8,128)(2,1)}, u32[]{:S(2)}) copy-start(bf16[4,128,2048]{2,1,0:T(8,128)(2,1)} %noise_ref.1) | copy-start | bytes 6291460
  0.6 41.2 %copy-start.1 = (f32[128,1024]{1,0:T(8,128)S(1)}, f32[128,1024]{1,0:T(8,128)}, u32[]{:S(2)}) copy-start(f32[128,1024]{1,0:T(8,128)} %states_ref.1) | copy-start | bytes 1572868
  0.7 41.2 %copy-start.4 = (s32[128]{0:T(128)S(1)}, s32[128]{0:T(128)}, u32[]{:S(2)}) copy-start(s32[128]{0:T(128)} %param.14) | copy-start | bytes 1540
  0.7 41.2 %copy-start.2 = (f32[2048]{0:T(1024)S(1)}, f32[2048]{0:T(1024)}, u32[]{:S(2)}) copy-start(f32[2048]{0:T(1024)} %param.12) | copy-start | bytes 24580
  0.7 41.2 %copy-start.3 = (f32[1024]{0:T(1024)S(1)}, f32[1024]{0:T(1024)}, u32[]{:S(2)}) copy-start(f32[1024]{0:T(1024)} %param.11) | copy-start | bytes 12292

commit v5 on v4

--- a/solution.py
+++ b/solution.py
@@ -12,6 +12,7 @@
 ROWS = 128
 GROUP = 4
 GROUPS = 32
+LINE = 8
 NARROW, WIDE = 8, 16
 SHIFT = 14
 CHAINS = 1 << SHIFT
@@ -54,7 +55,7 @@
     spill_ref,
     offset_ref,
     own_tickets,
-    group_tickets,
+    line_tickets,
     all_tickets,
     vis,
     pool,
@@ -90,7 +91,16 @@
     base = me - seat
     sibling = me + 1 - 2 * core
     partner = base + lax.rem(seat + 2, GROUP)
-    mates = [base + lax.rem(seat + i, GROUP) for i in range(1, GROUP)]
+    desk = lax.rem(me, LINE)
+    front = me - desk
+    mates = [front + lax.rem(desk + i, LINE) for i in range(1, LINE)]
+    far = (0, 1, 2, 1)
+    planes = [
+        LINE * (4 * lax.rem(gx + x, 4) + lax.rem(gz + z, 4)) + desk
+        for x, z in sorted(
+            ((x, z) for x in range(4) for z in range(4) if x + z), key=lambda d: -far[d[0]] - far[d[1]]
+        )
+    ]
 
     def away(i):
         x = lax.rem(gx + i // 8, 4)
@@ -101,10 +111,8 @@
         return (0, 1, 2, 1)[i // 8] + (0, 1, 2, 1)[i // 2 % 4] + i % 2
 
     order = sorted(range(1, GROUPS), key=hops, reverse=True)
-    rows = [away(i) for i in order]
 
     def everyone():
-        far = (0, 1, 2, 1)
         steps = [
             (x, z, y, c) for x in range(4) for z in range(4) for y in range(4) for c in range(2)
         ][1:]
@@ -116,7 +124,7 @@
         return [(xs[x] + zs[z] + ys[y], cs[c]) for x, z, y, c in steps]
 
     barrier = pltpu.get_barrier_semaphore()
-    for t in mates + rows:
+    for t in planes + mates:
         pl.semaphore_signal(barrier, inc=1, device_id=where_is(t), device_id_type=MESH)
 
     loads = [
@@ -136,7 +144,7 @@
     for copy in loads:
         copy.start()
     loads[0].wait()
-    group_tickets[pl.ds(seat, 1), :] = own_tickets[...]
+    line_tickets[pl.ds(desk, 1), :] = own_tickets[...]
     loads[1].wait()
 
     def block(owner, half=None):
@@ -146,11 +154,11 @@
         return pool.at[pl.ds(start, ROWS // 2)]
 
     pool[pl.ds(pl.multiple_of(seat * ROWS, ROWS), ROWS), :] = vis[...].astype(jnp.bfloat16)
-    pl.semaphore_wait(barrier, GROUP - 1 + GROUPS - 1)
+    pl.semaphore_wait(barrier, len(planes) + len(mates))
 
     for t in mates:
         remote(
-            own_tickets, group_tickets.at[pl.ds(seat, 1)], tick_sems.at[0], tick_sems.at[1], t
+            own_tickets, line_tickets.at[pl.ds(desk, 1)], tick_sems.at[0], tick_sems.at[1], t
         ).start()
     sends = []
 
@@ -164,16 +172,25 @@
     pass_on(seat, 1, ring_send.at[1], ring_recv.at[1], partner)
     pass_on(seat, None, pair_send.at[0], pair_recv, sibling)
 
-    wait_bytes(group_tickets.at[pl.ds(0, GROUP - 1)], tick_sems.at[1])
-    my_rows = pl.ds(pl.multiple_of(base, GROUP), GROUP)
-    all_tickets[my_rows, :] = group_tickets[...]
-    for t in rows:
+    wait_bytes(line_tickets.at[pl.ds(0, LINE - 1)], tick_sems.at[1])
+    my_rows = pl.ds(pl.multiple_of(front, LINE), LINE)
+    all_tickets[my_rows, :] = line_tickets[...]
+    for t in planes:
         remote(
-            group_tickets, all_tickets.at[my_rows], tick_sems.at[2], tick_sems.at[3], t
+            line_tickets, all_tickets.at[my_rows], tick_sems.at[2], tick_sems.at[3], t
         ).start()
 
+    lower = lax.broadcasted_iota(jnp.int32, (ROWS, ROWS), 0) <= lax.broadcasted_iota(
+        jnp.int32, (ROWS, ROWS), 1
+    )
+    mine = line_tickets[pl.ds(pl.multiple_of(desk - seat, GROUP), GROUP), :]
+    inner = jnp.dot(
+        mine.astype(jnp.float32).astype(jnp.bfloat16),
+        jnp.where(lower, 1.0, 0.0).astype(jnp.bfloat16),
+        preferred_element_type=jnp.float32,
+    )
     loads[6].wait()
-    wait_bytes(all_tickets.at[pl.ds(0, (GROUPS - 1) * GROUP)], tick_sems.at[3])
+    wait_bytes(all_tickets.at[pl.ds(0, ROWS - LINE)], tick_sems.at[3])
     device = lax.broadcasted_iota(jnp.int32, (ROWS, 1), 0)
     lane = lax.broadcasted_iota(jnp.int32, (1, ROWS), 1)
     everything = all_tickets[...].astype(jnp.float32)
@@ -204,15 +221,6 @@
     first = count(point(lane * ROWS + heir) < group_first, 1)
     place = first + (slot_row & (cap - 1))
     level = jnp.where(place < ROWS, point(place * ROWS + heir), jnp.int32(1 << 30))
-    lower = lax.broadcasted_iota(jnp.int32, (ROWS, ROWS), 0) <= lax.broadcasted_iota(
-        jnp.int32, (ROWS, ROWS), 1
-    )
-    mine = group_tickets[...]
-    inner = jnp.dot(
-        mine.astype(jnp.float32).astype(jnp.bfloat16),
-        jnp.where(lower, 1.0, 0.0).astype(jnp.bfloat16),
-        preferred_element_type=jnp.float32,
-    )
     opened = before
     for d in range(GROUP):
         high = (opened + inner[d : d + 1, :]).astype(jnp.int32)
@@ -227,17 +235,19 @@
         pass_on(opposite, half, pair_send.at[1 + half], pair_recv, sibling)
     wait_bytes(pool.at[pl.ds(0, 2 * ROWS)], pair_recv)
 
-    for part in range(0, GROUPS, ROWS // cap):
+    def ship(i):
+        remote(
+            outbox.at[pl.ds(i, 1)], inbox.at[pl.ds(group, 1)], rows_send, rows_recv, away(i)
+        ).start()
+
+    share = ROWS // cap
+    for part in range(0, GROUPS, share):
         chunk = slice(part * cap, part * cap + ROWS)
         picked = jnp.dot(onehot[chunk, :], pool[...], preferred_element_type=jnp.float32)
-        outbox[part : part + ROWS // cap] = picked.reshape(ROWS // cap, cap, 1024).astype(
-            jnp.bfloat16
-        )
+        outbox[part : part + share] = picked.reshape(share, cap, 1024).astype(jnp.bfloat16)
     inbox[pl.ds(group, 1)] = outbox[0:1]
-    for i, t in zip(order, rows):
-        remote(
-            outbox.at[pl.ds(i, 1)], inbox.at[pl.ds(group, 1)], rows_send, rows_recv, t
-        ).start()
+    for i in order:
+        ship(i)
 
     loads[2].wait()
 
@@ -331,8 +341,8 @@
 
     for copy in sends:
         copy.wait_send()
-    wait_bytes(group_tickets.at[pl.ds(0, GROUP - 1)], tick_sems.at[0])
-    wait_bytes(all_tickets.at[pl.ds(0, (GROUPS - 1) * GROUP)], tick_sems.at[2])
+    wait_bytes(line_tickets.at[pl.ds(0, LINE - 1)], tick_sems.at[0])
+    wait_bytes(all_tickets.at[pl.ds(0, ROWS - LINE)], tick_sems.at[2])
     wait_bytes(outbox.at[pl.ds(1, GROUPS - 1)], rows_send)
 
     wait_bytes(all_stats.at[pl.ds(0, ROWS - 1)], stat_sems.at[1])
@@ -378,7 +388,7 @@
         scratch_shapes=[
             pltpu.VMEM((1, 1), i32),
             pltpu.VMEM((1, ROWS), i32),
-            pltpu.VMEM((GROUP, ROWS), i32),
+            pltpu.VMEM((LINE, ROWS), i32),
             pltpu.VMEM((ROWS, ROWS), i32),
             pltpu.VMEM((ROWS, 1024), f32),
             pltpu.VMEM((GROUP * ROWS, 1024), b16),

time: 43.8 us -> 43 us (0.982)
  Pallas kernels: 40.5 us -> 39.7 us
    pallas_call x1, Pallas kernels: 39.7 us -> 38.9 us  [run(): pl.pallas_call(functools.partial(step_kernel, cap), out_shape=(jax.ShapeD...]
where the time goes in v5:
time: 43 us; the launch traced here: 42.3 us
  Pallas kernels  39.7 us (92%)
  between operations  2.32 us (5%)
    pallas_call x1, Pallas kernels, run(): pl.pallas_call(functools.partial(step_kernel, cap), out_shape=(jax.ShapeD...  38.9 us

profile of v5, /device:TPU:0, one launch (start us, length us, event | category | flops | bytes accessed | tf_op | source)
XLA Modules:
  0.0 42.3 jit_solution(12648849106761983513)
XLA Ops:
  0.6 0.0 copy-start
  0.6 0.0 copy-start.1
  0.7 0.0 copy-start.4
  0.7 0.0 copy-start.2
  0.7 0.0 copy-start.3
  1.5 38.9 %shard_map.94 = (f32[128,1024]{1,0:T(8,128)S(1)}, f32[1,256]{1,0:T(1,128)S(1)}, s32[1,1]{1,0:T(1,128)}) custom-call(f32[128,1024]{1,0:T(8,128)} %states_ref.1, bf16[1024,2048]{1,0:T(8,128)(2,1)} %coupling_ref.1, f32[1,1024]{1,0:T(1,128)} %bitcast.10, f32[1,2048]{1,0:T(1,128)} %bitcast.8, bf16[4,128,2048]{2,1,0:T(8,128)(2,1)} %noise_ref.1, ...), custom_call_target="tpu_custom_call" | custom-call | tf_op jit(solution)/shard_map/pallas_call | solution.py:375
  41.0 0.0 copy-done
  41.0 0.0 copy-done.1
  41.0 0.0 copy-done.4
  41.1 0.0 copy-done.2
  41.1 0.0 copy-done.3
  41.1 0.2 conditional.1
  41.3 0.8 %shard_map.95 = (f32[128,1024]{1,0:T(8,128)}, f32[1,128]{1,0:T(1,128)}, f32[1,1]{1,0:T(1,128)}) custom-call(f32[128,1024]{1,0:T(8,128)S(1)} %get-tuple-element.41.visible, f32[1,256]{1,0:T(1,128)S(1)} %get-tuple-element.42.small), custom_call_target="tpu_custom_call" | custom-call | tf_op jit(solution)/shard_map/pallas_call | solution.py:441
Async XLA Ops:
  0.6 40.4 %copy-start = (bf16[4,128,2048]{2,1,0:T(8,128)(2,1)S(1)}, bf16[4,128,2048]{2,1,0:T(8,128)(2,1)}, u32[]{:S(2)}) copy-start(bf16[4,128,2048]{2,1,0:T(8,128)(2,1)} %noise_ref.1) | copy-start | bytes 6291460
  0.6 40.4 %copy-start.1 = (f32[128,1024]{1,0:T(8,128)S(1)}, f32[128,1024]{1,0:T(8,128)}, u32[]{:S(2)}) copy-start(f32[128,1024]{1,0:T(8,128)} %states_ref.1) | copy-start | bytes 1572868
  0.7 40.4 %copy-start.4 = (s32[128]{0:T(128)S(1)}, s32[128]{0:T(128)}, u32[]{:S(2)}) copy-start(s32[128]{0:T(128)} %param.14) | copy-start | bytes 1540
  0.7 40.4 %copy-start.2 = (f32[2048]{0:T(1024)S(1)}, f32[2048]{0:T(1024)}, u32[]{:S(2)}) copy-start(f32[2048]{0:T(1024)} %param.12) | copy-start | bytes 24580
  0.7 40.4 %copy-start.3 = (f32[1024]{0:T(1024)S(1)}, f32[1024]{0:T(1024)}, u32[]{:S(2)}) copy-start(f32[1024]{0:T(1024)} %param.11) | copy-start | bytes 12292
